TPU v7x, 32 devices: a whole 2x2x4 slice. The times are simulated.
32 devices in a mesh: groups: 2 (over y), seq: 4 (over z), tensor: 4 (over x, core).
Axes of the slice: x: 2, y: 2, z: 4, core: 2. Of those that a mesh axis runs over, the one named last changes fastest.
Arguments:
- final_block_queries: bfloat16 [256, 8192], P(('groups', 'seq'), 'tensor'), parts along dimension 0, may hold values from -96 to 96
- final_block_keys: bfloat16 [256, 1024], P(('groups', 'seq'), 'tensor'), parts along dimension 0, may hold values from -16 to 16
- final_block_values: bfloat16 [256, 1024], P(('groups', 'seq'), 'tensor'), parts along dimension 0, may hold values from -6 to 6
- prompt_cached_keys: bfloat16 [12288, 1024], P(('groups', 'seq'), 'tensor'), parts along dimension 0, may hold values from -16 to 16
- prompt_cached_values: bfloat16 [12288, 1024], P(('groups', 'seq'), 'tensor'), parts along dimension 0, may hold values from -6 to 6
- paged_cache_pool: bfloat16 [256, 128, 2, 1024], P(('groups', 'seq'), None, None, 'tensor'), parts along dimension 0, may hold values from -16 to 16
- step_slot_queries: bfloat16 [32, 4, 8192], P(('groups', 'seq'), None, 'tensor'), parts along dimension 0, may hold values from -96 to 96
- step_token_keys: bfloat16 [32, 4, 1024], P(('groups', 'seq'), None, 'tensor'), parts along dimension 0, may hold values from -16 to 16
- step_token_values: bfloat16 [32, 4, 1024], P(('groups', 'seq'), None, 'tensor'), parts along dimension 0, may hold values from -6 to 6
- normed_step_inputs: bfloat16 [32, 4, 8192], P(('groups', 'seq'), None, 'tensor'), parts along dimension 0, may hold values from -6 to 6
- adapter_down_maps: bfloat16 [8192, 128], P('tensor'), may hold values from -0.0625 to 0.0625
- adapter_up_maps: bfloat16 [128, 8192], P(None, 'tensor'), may hold values from -1.5 to 1.5
- slot_request: int32 [32], P('groups'), parts along dimension 0, may hold values from 0 to 15, as said below
- request_page_table: int32 [32, 8], P('groups'), parts along dimension 0, may hold values from 0 to 127, as said below
- lengths: int32 [32], P('groups'), parts along dimension 0, may hold values from 2 to 1024, as said below
- request_adapter: int32 [32], P('groups'), parts along dimension 0, may hold values from 0 to 7
- request_rank: int32 [32], P('groups'), parts along dimension 0, may hold values from 4 to 16
Outputs:
- prefill_out: bfloat16 [256, 8192], P(('groups', 'seq'), 'tensor'), parts along dimension 0
- decode_out: bfloat16 [32, 4, 8192], P(('groups', 'seq'), None, 'tensor'), parts along dimension 0
There are 2 independent parts, one for each index of `groups`. A program takes and returns all parts, laid end to end along the dimension named above; an argument that names none is the same for every part. Nothing has to cross between parts.
Inputs may be any that keep to these rules, and one draw needn't show every extreme that they name: A permutation: slot k serves request slot_request[k]; the owner of slots k * 4 to (k + 1) * 4 - 1 is owner k. `request_page_table`: every pool page is named exactly once. For every owner and every block of 32 pool pages (pages b * 32 to (b + 1) * 32 - 1), exactly 8 of the pages of that owner's requests lie in the block. `lengths`: some request has exactly 1024 cached tokens.
All inputs are finite; a program needn't handle non-finite values.
Results may differ from a plain program's by a relative error of at most 0.028.
Values may be sent and summed in bfloat16 or wider, within the bound.
No kernel may reach another device: no remote copies, remote signals or barrier semaphores. Data moves between devices by JAX's collectives and lax.ppermute only.
A program may use at most 128 MiB of HBM per device.

v0:
```python
import jax
import jax.numpy as jnp
from jax import lax
from jax.sharding import PartitionSpec as P

HEAD_SIZE = 128
LARGEST_RANK = 16
MASKED = -1e30


def lookup_rows(lookup, positions):
    hit_mask = positions[..., None] == jnp.arange(lookup.shape[0], dtype=jnp.int32)
    if lookup.ndim == 1:
        return jnp.sum(jnp.where(hit_mask, lookup, 0), axis=-1)
    return jnp.sum(jnp.where(hit_mask[..., None], lookup, 0), axis=-2)


def partial_softmax(query_vectors, paged_key_rows, paged_value_rows, allowed):
    batch_count, query_total_count, query_width = query_vectors.shape
    kv_heads = paged_key_rows.shape[2] // HEAD_SIZE
    heads_per_group = query_width // HEAD_SIZE // kv_heads
    query_head_rows = query_vectors.reshape(
        batch_count, query_total_count, kv_heads, heads_per_group, HEAD_SIZE
    )
    key_head_rows = paged_key_rows.reshape(
        batch_count, paged_key_rows.shape[1], kv_heads, HEAD_SIZE
    )
    value_head_rows = paged_value_rows.reshape(
        batch_count, paged_value_rows.shape[1], kv_heads, HEAD_SIZE
    )
    scores = jnp.einsum(
        "etkgd,epkd->ekgtp", query_head_rows, key_head_rows, preferred_element_type=jnp.float32
    ) * HEAD_SIZE ** (-0.5)
    key_mask = allowed[:, None, None, :, :]
    scores = jnp.where(key_mask, scores, MASKED)
    row_max = jnp.max(scores, axis=-1)
    weights = jnp.where(key_mask, jnp.exp(scores - row_max[..., None]), 0.0)
    row_total = jnp.sum(weights, axis=-1)
    summed = jnp.einsum(
        "ekgtp,epkd->etkgd",
        weights.astype(jnp.bfloat16),
        value_head_rows,
        preferred_element_type=jnp.float32,
    )
    heads_here = kv_heads * heads_per_group
    row_max = jnp.transpose(row_max, (0, 3, 1, 2)).reshape(
        batch_count, query_total_count, heads_here
    )
    row_total = jnp.transpose(row_total, (0, 3, 1, 2)).reshape(
        batch_count, query_total_count, heads_here
    )
    return (
        summed.reshape(batch_count, query_total_count, heads_here, HEAD_SIZE),
        row_max,
        row_total,
    )


def combine(summed, row_max, row_total, along):
    best_max = jnp.max(row_max, axis=along, keepdims=True)
    factor = jnp.exp(row_max - best_max)
    whole_total = jnp.sum(factor * row_total, axis=along)
    merged = jnp.sum(factor[..., None] * summed, axis=along)
    return merged / whole_total[..., None]


def per_device(
    final_block_queries,
    final_block_keys,
    final_block_values,
    prompt_cached_keys,
    prompt_cached_values,
    paged_cache_pool,
    step_slot_queries,
    step_token_keys,
    step_token_values,
    normed_step_inputs,
    adapter_down_maps,
    adapter_up_maps,
    slot_request,
    request_page_table,
    lengths,
    request_adapter,
    request_rank,
):
    seq_count = lax.axis_size("seq")
    position = lax.axis_index("seq")
    span_rows = final_block_queries.shape[0]
    ctx_rows = prompt_cached_keys.shape[0]
    heads_here = final_block_queries.shape[1] // HEAD_SIZE
    everyone = lax.all_gather(final_block_queries, "seq", axis=0, tiled=True)
    span_total = everyone.shape[0]
    block_rows = min(128, span_total)
    paged_key_rows = jnp.concatenate([prompt_cached_keys, final_block_keys], axis=0)
    paged_value_rows = jnp.concatenate([prompt_cached_values, final_block_values], axis=0)
    spots = jnp.arange(paged_key_rows.shape[0], dtype=jnp.int32)
    key_pos = jnp.where(spots < ctx_rows, -1, position * span_rows + spots - ctx_rows)

    def run_block(row_start):
        query_rows = lax.dynamic_slice_in_dim(everyone, row_start, block_rows, 0)
        row_pos = row_start + jnp.arange(block_rows, dtype=jnp.int32)
        allowed = key_pos[None, :] <= row_pos[:, None]
        summed, row_max, row_total = partial_softmax(
            query_rows[None], paged_key_rows[None], paged_value_rows[None], allowed[None]
        )
        return (summed[0], row_max[0], row_total[0])

    starts = jnp.arange(span_total // block_rows, dtype=jnp.int32) * block_rows
    summed, row_max, row_total = lax.map(run_block, starts)
    summed = summed.reshape(span_total, heads_here, HEAD_SIZE)
    row_max = row_max.reshape(span_total, heads_here)
    row_total = row_total.reshape(span_total, heads_here)
    returned = (
        lax.all_to_all(summed, "seq", split_axis=0, concat_axis=0, tiled=True),
        lax.all_to_all(row_max, "seq", split_axis=0, concat_axis=0, tiled=True),
        lax.all_to_all(row_total, "seq", split_axis=0, concat_axis=0, tiled=True),
    )
    block_sums = returned[0].reshape(seq_count, span_rows, heads_here, HEAD_SIZE)
    block_maxes = returned[1].reshape(seq_count, span_rows, heads_here)
    block_totals = returned[2].reshape(seq_count, span_rows, heads_here)
    prefill_out = (
        combine(block_sums, block_maxes, block_totals, 0)
        .reshape(span_rows, heads_here * HEAD_SIZE)
        .astype(jnp.bfloat16)
    )
    slots_total = slot_request.shape[0]
    slots_here = slots_total // seq_count
    page_count = request_page_table.shape[1]
    pool_here = paged_cache_pool.shape[0]
    page_len = paged_cache_pool.shape[1]
    per_owner = slots_here * page_count // seq_count
    entries = slots_here * page_count
    decode_step_count = step_slot_queries.shape[1]
    slot_page_list = lookup_rows(request_page_table, slot_request)
    slot_length = lookup_rows(lengths, slot_request)
    owner_pages = slot_page_list.reshape(seq_count, entries)
    holder = owner_pages // pool_here
    pool_place = owner_pages % pool_here
    is_mine = holder == position
    rank_in = jnp.cumsum(is_mine.astype(jnp.int32), axis=1) - 1
    hit_mask = is_mine[:, :, None] & (rank_in[:, :, None] == jnp.arange(per_owner, dtype=jnp.int32))
    send_place = jnp.sum(jnp.where(hit_mask, pool_place[:, :, None], 0), axis=1).reshape(-1)
    entry_ids = jnp.arange(entries, dtype=jnp.int32)
    outgoing = paged_cache_pool[send_place]
    my_holder = lax.dynamic_index_in_dim(holder, position, 0, keepdims=False)
    before = (my_holder[None, :] == my_holder[:, None]) & (entry_ids[None, :] < entry_ids[:, None])
    arrive = my_holder * per_owner + jnp.sum(before.astype(jnp.int32), axis=1)
    my_requests = lax.dynamic_slice_in_dim(slot_request, position * slots_here, slots_here)
    my_lengths = lax.dynamic_slice_in_dim(slot_length, position * slots_here, slots_here)
    adapters = lookup_rows(request_adapter, my_requests)
    ranks = lookup_rows(request_rank, my_requests)
    hidden_input_rows = normed_step_inputs.reshape(
        slots_here * decode_step_count, normed_step_inputs.shape[2]
    )
    reduced_rank_state = lax.psum(
        jnp.dot(hidden_input_rows, adapter_down_maps, preferred_element_type=jnp.float32), "tensor"
    )
    column_indices = jnp.arange(adapter_down_maps.shape[1], dtype=jnp.int32)
    rank_keep_mask = (column_indices[None, :] // LARGEST_RANK == adapters[:, None]) & (
        column_indices[None, :] % LARGEST_RANK < ranks[:, None]
    )
    adapter_kept_rank = jnp.where(
        jnp.repeat(rank_keep_mask, decode_step_count, axis=0), reduced_rank_state, 0.0
    ).astype(jnp.bfloat16)
    raised_queries = jnp.dot(
        adapter_kept_rank, adapter_up_maps, preferred_element_type=jnp.float32
    ).reshape(slots_here, decode_step_count, -1)
    query_vectors = (step_slot_queries.astype(jnp.float32) + raised_queries).astype(jnp.bfloat16)
    step_pos = jnp.arange(decode_step_count, dtype=jnp.int32)
    fresh_ok = step_pos[None, :] <= step_pos[:, None]
    incoming = lax.all_to_all(outgoing, "seq", split_axis=0, concat_axis=0, tiled=True)
    gathered_pages = incoming[arrive].reshape(slots_here, page_count * page_len, 2, -1)
    all_keys = jnp.concatenate([gathered_pages[:, :, 0], step_token_keys], axis=1)
    all_values = jnp.concatenate([gathered_pages[:, :, 1], step_token_values], axis=1)
    cache_pos = jnp.arange(page_count * page_len, dtype=jnp.int32)
    cache_ok = jnp.broadcast_to(
        cache_pos[None, None, :] < my_lengths[:, None, None],
        (slots_here, decode_step_count, page_count * page_len),
    )
    allowed = jnp.concatenate(
        [
            cache_ok,
            jnp.broadcast_to(fresh_ok[None], (slots_here, decode_step_count, decode_step_count)),
        ],
        axis=2,
    )
    summed, row_max, row_total = partial_softmax(query_vectors, all_keys, all_values, allowed)
    decode_out = (
        (summed / row_total[..., None])
        .reshape(slots_here, decode_step_count, -1)
        .astype(jnp.bfloat16)
    )
    return (prefill_out, decode_out)


def solution(mesh):
    placed = (
        P(("groups", "seq"), "tensor"),
        P(("groups", "seq"), "tensor"),
        P(("groups", "seq"), "tensor"),
        P(("groups", "seq"), "tensor"),
        P(("groups", "seq"), "tensor"),
        P(("groups", "seq"), None, None, "tensor"),
        P(("groups", "seq"), None, "tensor"),
        P(("groups", "seq"), None, "tensor"),
        P(("groups", "seq"), None, "tensor"),
        P(("groups", "seq"), None, "tensor"),
        P("tensor", None),
        P(None, "tensor"),
        P("groups"),
        P("groups", None),
        P("groups"),
        P("groups"),
        P("groups"),
    )
    return jax.shard_map(
        per_device,
        mesh=mesh,
        in_specs=placed,
        out_specs=(P(("groups", "seq"), "tensor"), P(("groups", "seq"), None, "tensor")),
        check_vma=False,
    )
```

profile of v0, /device:TPU:0, one launch (start us, length us, event | category | flops | bytes accessed | tf_op | source)
XLA Modules:
  0.0 200.9 jit_solution(16508769630650685992)
XLA Ops:
  0.7 0.3 iota_compare_fusion
  0.9 1.2 pad_maximum_fusion
  2.2 0.7 copy.124
  2.8 17.6 %all_gather.3 = bf16[128,2048]{1,0:T(8,128)(2,1)S(1)} all-gather(bf16[32,2048]{1,0:T(8,128)(2,1)} %param.17), channel_id=1, replica_groups=mesh['groups'=2,'seq'=4,'tensor'=4] {'seq'}, dimensions={0}, use_global_device_ids=true | all-gather | bytes 655360 | tf_op jit(solution)/shard_map/all_gather | solution.py:91
  20.4 0.3 copy.125
  20.7 2.0 %fusion.1 = (f32[2,8,128]{2,1,0:T(8,128)S(1)}, f32[2,1568,128,8]{2,1,3,0:T(8,128)S(1)}) fusion(pred[128,1568]{0,1:T(8,128)(4,1)S(1)} %iota_compare_fusion, bf16[1568,2,128,1]{0,2,3,1:T(8,128)(2,1)S(1)} %bitcast.128, bf16[128,2,8,128]{0,3,2,1:T(8,128)(2,1)S(1)} %bitcast.129), kind=kOutput, calls=%fused_computation.5 | convolution fusion | flops 831715328 | bytes 14381056 | tf_op jit(solution)/shard_map/while/body/eval_jaxpr/etkgd,epkd->ekgtp/dot_general | solution.py:31
  22.8 3.0 %fusion.2 = f32[2,8,128]{2,1,0:T(8,128)S(1)} fusion(f32[2,1568,128,8]{2,1,3,0:T(8,128)S(1)} %get-tuple-element.36, f32[2,8,128]{2,1,0:T(8,128)S(1)} %get-tuple-element.35, pred[128,1568]{0,1:T(8,128)(4,1)S(1)} %iota_compare_fusion), kind=kLoop, calls=%fused_computation.6 | loop fusion | flops 16054272 | bytes 13062144 | tf_op jit(solution)/shard_map/while/body/eval_jaxpr/reduce_sum | solution.py:38
  25.8 1.5 copy-done.1
  27.4 0.7 reshape.433
  28.1 5.4 %all-to-all-start.2 = ((f32[4,1,512]{2,1,0:T(1,128)}), f32[4,1,512]{2,1,0:T(1,128)S(1)}, u32[]{:S(2)}, u32[]{:S(2)}) async-start(f32[4,1,512]{2,1,0:T(1,128)} %reshape.433), calls=%async_computation.2 | async-start | bytes 16384 | tf_op jit(solution)/shard_map/all_to_all | solution.py:116
  33.7 0.7 reshape.431
  34.4 0.7 copy.130
  35.0 4.1 %all-to-all-done.2 = f32[4,1,512]{2,1,0:T(1,128)S(1)} async-done(((f32[4,1,512]{2,1,0:T(1,128)}), f32[4,1,512]{2,1,0:T(1,128)S(1)}, u32[]{:S(2)}, u32[]{:S(2)}) %all-to-all-start.2) | async-done | bytes 8224 | tf_op jit(solution)/shard_map/all_to_all | solution.py:116
  39.1 3.2 %all-to-all-start = ((f32[4,1,512]{2,1,0:T(1,128)}), f32[4,1,512]{2,1,0:T(1,128)S(1)}, u32[]{:S(2)}, u32[]{:S(2)}) async-start(f32[4,1,512]{2,1,0:T(1,128)} %reshape.431), calls=%async_computation | async-start | bytes 16384 | tf_op jit(solution)/shard_map/all_to_all | solution.py:115
  42.4 6.5 %fusion.5 = f32[2,128,8,128]{3,1,2,0:T(8,128)S(1)} fusion(bf16[1568,2,128,1]{0,2,3,1:T(8,128)(2,1)S(1)} %bitcast.131, f32[2,1568,128,8]{2,1,3,0:T(8,128)} %copy-done.1, f32[2,8,128]{2,1,0:T(8,128)S(1)} %get-tuple-element.35, pred[128,1568]{0,1:T(8,128)(4,1)S(1)} %iota_compare_fusion), kind=kOutput, calls=%fused_computation.9 | convolution fusion | flops 838139904 | bytes 14905344 | tf_op jit(solution)/shard_map/while/body/eval_jaxpr/ekgtp,epkd->etkgd/dot_general | solution.py:39
  48.9 1.4 copy.132
  50.3 5.0 %all-to-all-start.1 = ((f32[128,16,128]{2,1,0:T(8,128)}), f32[128,16,128]{2,1,0:T(8,128)S(1)}, u32[]{:S(2)}, u32[]{:S(2)}) async-start(f32[128,16,128]{2,1,0:T(8,128)} %copy.132), calls=%async_computation.1 | async-start | bytes 2097152 | tf_op jit(solution)/shard_map/all_to_all | solution.py:114
  55.4 0.4 select_reduce_fusion
  55.8 0.2 reduce_window_sum.11
  56.1 0.1 select_reduce_fusion.1
  56.3 12.3 %gather_fusion = bf16[32,128,2,256]{3,2,1,0:T(2,128)(2,1)} fusion(bf16[32,128,2,256]{3,2,1,0:T(2,128)(2,1)} %param.22, s32[1024]{0:T(1024)S(1)} %pad_clamp_fusion.1), kind=kCustom, calls=%fused_computation | custom fusion | bytes 8388736 | tf_op jit(solution)/shard_map/gather | solution.py:144
  68.7 7.4 %all-to-all-done.1 = f32[128,16,128]{2,1,0:T(8,128)S(1)} async-done(((f32[128,16,128]{2,1,0:T(8,128)}), f32[128,16,128]{2,1,0:T(8,128)S(1)}, u32[]{:S(2)}, u32[]{:S(2)}) %all-to-all-start.1) | async-done | bytes 1048608 | tf_op jit(solution)/shard_map/all_to_all | solution.py:114
  76.0 5.0 %all-to-all-start.3 = ((bf16[32,128,2,256]{3,2,1,0:T(2,128)(2,1)}), bf16[32,128,2,256]{3,2,1,0:T(2,128)(2,1)}, u32[]{:S(2)}, u32[]{:S(2)}) async-start(bf16[32,128,2,256]{3,2,1,0:T(2,128)(2,1)} %gather_fusion), calls=%async_computation.3 | async-start | bytes 8388608 | tf_op jit(solution)/shard_map/all_to_all | solution.py:171
  81.2 0.2 fusion.49
  81.4 5.8 %psum.7 = bf16[16,128]{1,0:T(8,128)(2,1)S(1)} all-reduce(f32[16,128]{1,0:T(8,128)S(1)} %fusion.49), channel_id=1, replica_groups=mesh['groups'=2,'seq'=4,'tensor'=4] {'tensor'}, use_global_device_ids=true, to_apply=%region_12.13 | all-reduce | flops 2048 | bytes 12288 | tf_op jit(solution)/shard_map/psum | solution.py:155
  87.2 0.2 select_reduce_fusion.4
  87.4 0.2 fusion.28
  87.8 0.2 select_reduce_fusion.2
  88.1 0.2 convert_reduce_fusion
  88.4 0.5 broadcast.338
  88.9 0.7 reduce.4
  89.7 0.7 reduce.3
  90.6 0.3 multiply_reduce_fusion
  91.0 0.1 divide_convert_fusion
  91.1 0.7 copy.168
  91.8 78.9 %all-to-all-done.3 = bf16[32,128,2,256]{3,2,1,0:T(2,128)(2,1)} async-done(((bf16[32,128,2,256]{3,2,1,0:T(2,128)(2,1)}), bf16[32,128,2,256]{3,2,1,0:T(2,128)(2,1)}, u32[]{:S(2)}, u32[]{:S(2)}) %all-to-all-start.3) | async-done | bytes 4194336 | tf_op jit(solution)/shard_map/all_to_all | solution.py:171
  170.8 5.0 %copy.136 = bf16[32,128,2,256]{3,1,2,0:T(8,128)(2,1)} copy(bf16[32,128,2,256]{3,2,1,0:T(2,128)(2,1)} %all-to-all-done.3) | data formatting | bytes 8388608 | tf_op jit(solution)/shard_map/all_to_all | solution.py:171
  175.8 4.9 %gather_fusion.1 = bf16[32,128,2,256]{3,1,2,0:T(8,128)(2,1)} fusion(bf16[32,128,2,256]{3,1,2,0:T(8,128)(2,1)} %copy.136, s32[1024]{0:T(1024)S(1)} %pad_clamp_fusion), kind=kCustom, calls=%fused_computation.1 | custom fusion | bytes 8388736 | tf_op jit(solution)/shard_map/gather | solution.py:172
  180.7 2.5 %copy.137 = bf16[32,128,2,256]{3,1,0,2:T(8,128)(2,1)S(1)} copy(bf16[32,128,2,256]{3,1,2,0:T(8,128)(2,1)} %gather_fusion.1) | data formatting | bytes 8388608 | tf_op jit(solution)/shard_map/gather | solution.py:172
  183.2 2.3 %fusion.45 = (bf16[4,1024,1,256]{3,1,0,2:T(8,128)(2,1)}, bf16[4,1024,1,256]{3,1,0,2:T(8,128)(2,1)}) fusion(bf16[4,1024,2,256]{3,1,0,2:T(8,128)(2,1)S(1)} %bitcast.124), kind=kLoop, calls=%fused_computation.94 | loop fusion | bytes 8388608 | tf_op jit(solution)/shard_map/slice | solution.py:173
  185.5 3.0 %copy.140 = bf16[4,1024,1,256]{1,3,0,2:T(8,128)(2,1)S(1)} copy(bf16[4,1024,1,256]{3,1,0,2:T(8,128)(2,1)} %get-tuple-element.33) | data formatting | bytes 4194304 | tf_op jit(solution)/shard_map/slice | solution.py:173
  188.4 2.6 %copy.141 = bf16[4,1024,2,128]{3,1,2,0:T(8,128)(2,1)} copy(bf16[4,1024,2,128]{1,3,2,0:T(8,128)(2,1)S(1)} %bitcast.125) | data formatting | bytes 4194304 | tf_op jit(solution)/shard_map/concatenate | solution.py:173
  191.0 3.0 %copy.138 = bf16[4,1024,1,256]{1,3,0,2:T(8,128)(2,1)S(1)} copy(bf16[4,1024,1,256]{3,1,0,2:T(8,128)(2,1)} %get-tuple-element.34) | data formatting | bytes 4194304 | tf_op jit(solution)/shard_map/slice | solution.py:174
  194.0 2.6 %copy.139 = bf16[4,1024,2,128]{3,1,2,0:T(8,128)(2,1)} copy(bf16[4,1024,2,128]{1,3,2,0:T(8,128)(2,1)S(1)} %bitcast.126) | data formatting | bytes 4194304 | tf_op jit(solution)/shard_map/concatenate | solution.py:174
  196.6 2.7 %fusion.46 = (f32[4,2,8,4]{2,3,1,0:T(4,128)S(1)}, bf16[4,2,8,4,1028]{4,2,3,1,0:T(8,128)(2,1)S(1)}) fusion(bf16[4,4,2,128]{3,1,2,0:T(4,128)(2,1)S(1)} %bitcast.140, bf16[4,1024,2,128]{3,1,2,0:T(8,128)(2,1)} %copy.141, pred[4,4,1028]{2,1,0:T(4,128)(4,1)S(1)} %pad_add_fusion, bf16[4,4,2,8,128]{4,3,2,1,0:T(8,128)(2,1)S(1)} %reshape.409), kind=kOutput, calls=%fused_computation.95 | convolution fusion | flops 73161728 | bytes 2714688 | tf_op jit(solution)/shard_map/sub | solution.py:37
  199.4 0.5 fusion.18
  200.0 0.1 div.52
  200.2 0.7 divide_convert_fusion.1
  (71 shorter events, 1.7 us)
Async XLA Ops:
  0.6 86.8 %copy-start = (bf16[128,2048]{1,0:T(8,128)(2,1)S(1)}, bf16[128,2048]{1,0:T(8,128)(2,1)}, u32[]{:S(2)}) copy-start(bf16[128,2048]{1,0:T(8,128)(2,1)} %param.28) | copy-start | bytes 1572868
  22.7 4.6 %copy-start.1 = (f32[2,1568,128,8]{2,1,3,0:T(8,128)}, f32[2,1568,128,8]{2,1,3,0:T(8,128)S(1)}, u32[]{:S(2)}) copy-start(f32[2,1568,128,8]{2,1,3,0:T(8,128)S(1)} %get-tuple-element.36) | copy-start | bytes 38535172
  22.8 10.8 %copy-start.3 = (bf16[1536,256]{1,0:T(8,128)(2,1)S(1)}, bf16[1536,256]{1,0:T(8,128)(2,1)}, u32[]{:S(2)}) copy-start(bf16[1536,256]{1,0:T(8,128)(2,1)} %param.21) | copy-start | bytes 2359300
  22.8 10.8 %copy-start.7 = (bf16[32,256]{1,0:T(8,128)(2,1)S(1)}, bf16[32,256]{1,0:T(8,128)(2,1)}, u32[]{:S(2)}) copy-start(bf16[32,256]{1,0:T(8,128)(2,1)} %param.19) | copy-start | bytes 49156
  28.1 11.0 %all-to-all-start.2 = ((f32[4,1,512]{2,1,0:T(1,128)}), f32[4,1,512]{2,1,0:T(1,128)S(1)}, u32[]{:S(2)}, u32[]{:S(2)}) async-start(f32[4,1,512]{2,1,0:T(1,128)} %reshape.433), calls=%async_computation.2 | async-start | bytes 16384 | tf_op jit(solution)/shard_map/all_to_all | solution.py:116
  39.1 11.1 %all-to-all-start = ((f32[4,1,512]{2,1,0:T(1,128)}), f32[4,1,512]{2,1,0:T(1,128)S(1)}, u32[]{:S(2)}, u32[]{:S(2)}) async-start(f32[4,1,512]{2,1,0:T(1,128)} %reshape.431), calls=%async_computation | async-start | bytes 16384 | tf_op jit(solution)/shard_map/all_to_all | solution.py:115
  48.8 6.5 %copy-start.11 = (s32[16]{0:T(128)S(1)}, s32[16]{0:T(128)}, u32[]{:S(2)}) copy-start(s32[16]{0:T(128)} %param.29) | copy-start | bytes 196
  48.8 6.5 %copy-start.8 = (s32[16,8]{0,1:T(8,128)S(1)}, s32[16,8]{0,1:T(8,128)}, u32[]{:S(2)}) copy-start(s32[16,8]{0,1:T(8,128)} %param.30) | copy-start | bytes 1540
  50.3 25.8 %all-to-all-start.1 = ((f32[128,16,128]{2,1,0:T(8,128)}), f32[128,16,128]{2,1,0:T(8,128)S(1)}, u32[]{:S(2)}, u32[]{:S(2)}) async-start(f32[128,16,128]{2,1,0:T(8,128)} %copy.132), calls=%async_computation.1 | async-start | bytes 2097152 | tf_op jit(solution)/shard_map/all_to_all | solution.py:114
  68.6 12.5 %copy-start.5 = (bf16[4,4,2048]{2,1,0:T(4,128)(2,1)S(1)}, bf16[4,4,2048]{2,1,0:T(4,128)(2,1)}, u32[]{:S(2)}) copy-start(bf16[4,4,2048]{2,1,0:T(4,128)(2,1)} %param.26) | copy-start | bytes 196612
  68.6 12.5 %copy-start.4 = (bf16[2048,128]{1,0:T(8,128)(2,1)S(1)}, bf16[2048,128]{1,0:T(8,128)(2,1)}, u32[]{:S(2)}) copy-start(bf16[2048,128]{1,0:T(8,128)(2,1)} %param.27) | copy-start | bytes 1572868
  68.6 18.5 %copy-start.9 = (s32[16]{0:T(128)S(1)}, s32[16]{0:T(128)}, u32[]{:S(2)}) copy-start(s32[16]{0:T(128)} %param.32) | copy-start | bytes 196
  68.7 18.5 %copy-start.10 = (s32[16]{0:T(128)S(1)}, s32[16]{0:T(128)}, u32[]{:S(2)}) copy-start(s32[16]{0:T(128)} %param.33) | copy-start | bytes 196
  68.7 19.0 %copy-start.6 = (bf16[4,4,2048]{2,1,0:T(4,128)(2,1)S(1)}, bf16[4,4,2048]{2,1,0:T(4,128)(2,1)}, u32[]{:S(2)}) copy-start(bf16[4,4,2048]{2,1,0:T(4,128)(2,1)} %param.23) | copy-start | bytes 196612
  68.7 19.1 %copy-start.14 = (s32[16]{0:T(128)S(1)}, s32[16]{0:T(128)}, u32[]{:S(2)}) copy-start(s32[16]{0:T(128)} %param.31) | copy-start | bytes 196
  76.0 94.7 %all-to-all-start.3 = ((bf16[32,128,2,256]{3,2,1,0:T(2,128)(2,1)}), bf16[32,128,2,256]{3,2,1,0:T(2,128)(2,1)}, u32[]{:S(2)}, u32[]{:S(2)}) async-start(bf16[32,128,2,256]{3,2,1,0:T(2,128)(2,1)} %gather_fusion), calls=%async_computation.3 | async-start | bytes 8388608 | tf_op jit(solution)/shard_map/all_to_all | solution.py:171
  191.0 5.6 %copy-start.12 = (bf16[4,4,256]{2,1,0:T(4,128)(2,1)S(1)}, bf16[4,4,256]{2,1,0:T(4,128)(2,1)}, u32[]{:S(2)}) copy-start(bf16[4,4,256]{2,1,0:T(4,128)(2,1)} %param.24) | copy-start | bytes 24580
  196.6 2.7 %copy-start.2 = (bf16[4,1024,2,128]{3,1,2,0:T(8,128)(2,1)S(1)}, bf16[4,1024,2,128]{3,1,2,0:T(8,128)(2,1)}, u32[]{:S(2)}) copy-start(bf16[4,1024,2,128]{3,1,2,0:T(8,128)(2,1)} %copy.139) | copy-start | bytes 6291460
  196.6 2.7 %copy-start.13 = (bf16[4,4,256]{2,1,0:T(4,128)(2,1)S(1)}, bf16[4,4,256]{2,1,0:T(4,128)(2,1)}, u32[]{:S(2)}) copy-start(bf16[4,4,256]{2,1,0:T(4,128)(2,1)} %param.25) | copy-start | bytes 24580
where the time goes:
time: 202 us; the launch traced here: 201 us
  waiting for transfers between devices  90.4 us (45%)
  local copies, waits for them, and re-layouts  46.6 us (23%)
  blocking collectives  23.3 us (12%)
  starting transfers between devices  18.7 us (9%)
  matrix products  12.1 us (6%)
  other arithmetic  8.73 us (4%)
    all_to_all x1, waiting for transfers between devices, per_device(): lax.all_to_all(outgoing, 'seq', split_axis=0, concat_axis=0, tiled=True)  78.9 us
    all_gather x1, blocking collectives, per_device(): everyone = lax.all_gather(final_block_queries, 'seq', axis=0, tiled=True)  17.6 us
    gather x1, local copies, waits for them, and re-layouts, per_device(): outgoing = paged_cache_pool[send_place]  12.3 us
    gather x2, local copies, waits for them, and re-layouts, per_device(): incoming[arrive].reshape(slots_here, page_count * page_len, 2, -1)  7.38 us
    all_to_all x1, waiting for transfers between devices, per_device(): lax.all_to_all(summed, 'seq', split_axis=0, concat_axis=0, tiled=True)  7.36 us
    dot_general x2, matrix products, partial_softmax(): jnp.einsum('ekgtp,epkd->etkgd', weights.astype(jnp.bfloat16), value_head_...  6.91 us
    psum x1, blocking collectives, per_device(): lax.psum(jnp.dot(hidden_input_rows, adapter_down_maps, preferred_element_...  5.75 us
    all_to_all x1, starting transfers between devices, per_device(): lax.all_to_all(row_total, 'seq', split_axis=0, concat_axis=0, tiled=True)  5.39 us
  transfers between devices with their start and end apart: 4, of which 3 were waited for; matrix products, arithmetic and copies ran while one was open for 14% of the time, Pallas kernels for 0%

commit v1 on v0

--- a/solution.py
+++ b/solution.py
@@ -88,7 +88,18 @@
     span_rows = final_block_queries.shape[0]
     ctx_rows = prompt_cached_keys.shape[0]
     heads_here = final_block_queries.shape[1] // HEAD_SIZE
-    everyone = lax.all_gather(final_block_queries, "seq", axis=0, tiled=True)
+    ways = lax.axis_size("seq")
+    up = [(d, (d + 1) % ways) for d in range(ways)]
+    down = [(d, (d - 1) % ways) for d in range(ways)]
+    earlier, later = ([final_block_queries], [final_block_queries])
+    for _ in range(ways // 2):
+        earlier.append(lax.ppermute(earlier[-1], "seq", up))
+    for _ in range((ways - 1) // 2):
+        later.append(lax.ppermute(later[-1], "seq", down))
+    line = jnp.concatenate([*earlier[::-1], *later[1:]], axis=0)
+    everyone = jnp.roll(
+        line, (lax.axis_index("seq") - ways // 2) * final_block_queries.shape[0], axis=0
+    )
     span_total = everyone.shape[0]
     block_rows = min(128, span_total)
     paged_key_rows = jnp.concatenate([prompt_cached_keys, final_block_keys], axis=0)

time: 202 us -> 228 us (1.13)
  waiting for transfers between devices: 90.4 us -> 125 us
  blocking collectives: 23.3 us -> 5.75 us
  local copies, waits for them, and re-layouts: 46.6 us -> 52.9 us
  starting transfers between devices: 18.7 us -> 21.6 us
    ppermute x0 -> x3, waiting for transfers between devices: none -> 32.3 us  [the longest x2 24.2 us: per_device(): earlier.append(lax.ppermute(earlier[-1], 'seq', up))]
    all_gather x1 -> x0, blocking collectives: 17.6 us -> none  [per_device(): everyone = lax.all_gather(final_block_queries, 'seq', axis=0, tiled=True)]
    ppermute x0 -> x3, starting transfers between devices: none -> 5.2 us  [the longest x2 3.11 us: per_device(): earlier.append(lax.ppermute(earlier[-1], 'seq', up))]
    concatenate x0 -> x1, local copies, waits for them, and re-layouts: none -> 5.11 us  [per_device(): jnp.roll(line, (lax.axis_index('seq') - ways // 2) * final_block_queries....]
    unnamed x35 -> x36, local copies, waits for them, and re-layouts: 3.81 us -> 5.05 us
  transfers between devices with their start and end apart: 4 -> 7, of which waited for: 3 -> 6; matrix products, arithmetic and copies ran while one was open for 14% -> 13% of each run, Pallas kernels for 0% -> 0%
where the time goes in v1:
time: 228 us; the launch traced here: 227 us
  waiting for transfers between devices  125 us (55%)
  local copies, waits for them, and re-layouts  52.9 us (23%)
  starting transfers between devices  21.6 us (9%)
  matrix products  12.1 us (5%)
  other arithmetic  8.73 us (4%)
  blocking collectives  5.75 us (3%)
    all_to_all x1, waiting for transfers between devices, per_device(): lax.all_to_all(outgoing, 'seq', split_axis=0, concat_axis=0, tiled=True)  80.4 us
    ppermute x2, waiting for transfers between devices, per_device(): earlier.append(lax.ppermute(earlier[-1], 'seq', up))  24.2 us
    gather x1, local copies, waits for them, and re-layouts, per_device(): outgoing = paged_cache_pool[send_place]  12.3 us
    all_to_all x1, waiting for transfers between devices, per_device(): lax.all_to_all(summed, 'seq', split_axis=0, concat_axis=0, tiled=True)  8.36 us
    ppermute x1, waiting for transfers between devices, per_device(): later.append(lax.ppermute(later[-1], 'seq', down))  8.11 us
    gather x2, local copies, waits for them, and re-layouts, per_device(): incoming[arrive].reshape(slots_here, page_count * page_len, 2, -1)  7.38 us
    dot_general x2, matrix products, partial_softmax(): jnp.einsum('ekgtp,epkd->etkgd', weights.astype(jnp.bfloat16), value_head_...  6.91 us
    psum x1, blocking collectives, per_device(): lax.psum(jnp.dot(hidden_input_rows, adapter_down_maps, preferred_element_...  5.75 us
  transfers between devices with their start and end apart: 7, of which 6 were waited for; matrix products, arithmetic and copies ran while one was open for 13% of the time, Pallas kernels for 0%

profile of v1, /device:TPU:0, one launch (start us, length us, event | category | flops | bytes accessed | tf_op | source)
XLA Modules:
  0.0 227.2 jit_solution(6373391852047155564)
XLA Ops:
  0.6 1.2 copy.143
  1.9 3.1 %collective-permute-start = (bf16[32,2048]{0,1:T(8,128)(2,1)S(1)}, bf16[32,2048]{0,1:T(8,128)(2,1)}, u32[]{:S(2)}, u32[]{:S(2)}) collective-permute-start(bf16[32,2048]{0,1:T(8,128)(2,1)S(1)} %copy.143), channel_id=1, source_target_pairs={{0,4},{4,8},{8,12},{12,0},{1,5},{5,9},{9,13},{13,1},{2,6},{6,10},{... | collective-permute-start | bytes 393224 | tf_op jit(solution)/shard_map/ppermute | solution.py:96
  5.0 2.1 collective-permute-start.2
  7.1 0.3 iota_compare_fusion
  7.4 12.6 %collective-permute-done = bf16[32,2048]{0,1:T(8,128)(2,1)} collective-permute-done((bf16[32,2048]{0,1:T(8,128)(2,1)S(1)}, bf16[32,2048]{0,1:T(8,128)(2,1)}, u32[]{:S(2)}, u32[]{:S(2)}) %collective-permute-start) | collective-permute-done | bytes 131104 | tf_op jit(solution)/shard_map/ppermute | solution.py:96
  19.9 1.2 pad_maximum_fusion
  21.2 0.7 copy.142
  21.8 8.1 %collective-permute-done.2 = bf16[32,2048]{0,1:T(8,128)(2,1)} collective-permute-done((bf16[32,2048]{0,1:T(8,128)(2,1)S(1)}, bf16[32,2048]{0,1:T(8,128)(2,1)}, u32[]{:S(2)}, u32[]{:S(2)}) %collective-permute-start.2) | collective-permute-done | bytes 131104 | tf_op jit(solution)/shard_map/ppermute | solution.py:98
  29.9 11.6 %collective-permute-done.1 = bf16[32,2048]{0,1:T(8,128)(2,1)} collective-permute-done((bf16[32,2048]{0,1:T(8,128)(2,1)}, bf16[32,2048]{0,1:T(8,128)(2,1)}, u32[]{:S(2)}, u32[]{:S(2)}) %collective-permute-start.1) | collective-permute-done | bytes 131104 | tf_op jit(solution)/shard_map/ppermute | solution.py:96
  41.6 5.1 %concatenate.32 = bf16[256,2048]{0,1:T(8,128)(2,1)S(1)} concatenate(bf16[32,2048]{0,1:T(8,128)(2,1)} %collective-permute-done.1, bf16[32,2048]{0,1:T(8,128)(2,1)} %collective-permute-done, bf16[32,2048]{0,1:T(8,128)(2,1)S(1)} %copy.143, bf16[32,2048]{0,1:T(8,128)(2,1)} %collective-permute-done.2, bf16[32,2048]{0,1:T(8,128)(2,1)} %collective-permute-done.1, ...), dimensions={0} | concatenate | bytes 2097152 | tf_op jit(solution)/shard_map/jit(_roll_dynamic)/concatenate | solution.py:100
  46.7 0.2 constant_dynamic-slice_fusion.1
  46.9 2.0 fusion.1
  49.0 3.0 %fusion.2 = f32[2,8,128]{2,1,0:T(8,128)S(1)} fusion(f32[2,1568,128,8]{2,1,3,0:T(8,128)S(1)} %get-tuple-element.36, f32[2,8,128]{2,1,0:T(8,128)S(1)} %get-tuple-element.35, pred[128,1568]{0,1:T(8,128)(4,1)S(1)} %iota_compare_fusion), kind=kLoop, calls=%fused_computation.6 | loop fusion | flops 16054272 | bytes 13062144 | tf_op jit(solution)/shard_map/while/body/eval_jaxpr/reduce_sum | solution.py:38
  52.0 1.5 copy-done.1
  53.7 0.7 reshape.433
  54.3 3.2 %all-to-all-start.2 = ((f32[4,1,512]{2,1,0:T(1,128)}), f32[4,1,512]{2,1,0:T(1,128)S(1)}, u32[]{:S(2)}, u32[]{:S(2)}) async-start(f32[4,1,512]{2,1,0:T(1,128)} %reshape.433), calls=%async_computation.2 | async-start | bytes 16384 | tf_op jit(solution)/shard_map/all_to_all | solution.py:127
  57.7 0.7 copy.151
  58.5 0.7 reshape.431
  59.1 4.0 %all-to-all-done.2 = f32[4,1,512]{2,1,0:T(1,128)S(1)} async-done(((f32[4,1,512]{2,1,0:T(1,128)}), f32[4,1,512]{2,1,0:T(1,128)S(1)}, u32[]{:S(2)}, u32[]{:S(2)}) %all-to-all-start.2) | async-done | bytes 8224 | tf_op jit(solution)/shard_map/all_to_all | solution.py:127
  63.2 3.2 %all-to-all-start = ((f32[4,1,512]{2,1,0:T(1,128)}), f32[4,1,512]{2,1,0:T(1,128)S(1)}, u32[]{:S(2)}, u32[]{:S(2)}) async-start(f32[4,1,512]{2,1,0:T(1,128)} %reshape.431), calls=%async_computation | async-start | bytes 16384 | tf_op jit(solution)/shard_map/all_to_all | solution.py:126
  66.4 6.5 %fusion.5 = f32[2,128,8,128]{3,1,2,0:T(8,128)S(1)} fusion(bf16[1568,2,128,1]{0,2,3,1:T(8,128)(2,1)S(1)} %bitcast.131, f32[2,1568,128,8]{2,1,3,0:T(8,128)} %copy-done.1, f32[2,8,128]{2,1,0:T(8,128)S(1)} %get-tuple-element.35, pred[128,1568]{0,1:T(8,128)(4,1)S(1)} %iota_compare_fusion), kind=kOutput, calls=%fused_computation.9 | convolution fusion | flops 838139904 | bytes 14905344 | tf_op jit(solution)/shard_map/while/body/eval_jaxpr/ekgtp,epkd->etkgd/dot_general | solution.py:39
  72.9 1.4 copy.153
  74.3 5.0 %all-to-all-start.1 = ((f32[128,16,128]{2,1,0:T(8,128)}), f32[128,16,128]{2,1,0:T(8,128)S(1)}, u32[]{:S(2)}, u32[]{:S(2)}) async-start(f32[128,16,128]{2,1,0:T(8,128)} %copy.153), calls=%async_computation.1 | async-start | bytes 2097152 | tf_op jit(solution)/shard_map/all_to_all | solution.py:125
  79.4 0.4 select_reduce_fusion
  79.9 0.2 reduce_window_sum.11
  80.4 12.3 %gather_fusion = bf16[32,128,2,256]{3,2,1,0:T(2,128)(2,1)} fusion(bf16[32,128,2,256]{3,2,1,0:T(2,128)(2,1)} %param.22, s32[1024]{0:T(1024)S(1)} %pad_clamp_fusion.1), kind=kCustom, calls=%fused_computation | custom fusion | bytes 8388736 | tf_op jit(solution)/shard_map/gather | solution.py:155
  92.7 8.4 %all-to-all-done.1 = f32[128,16,128]{2,1,0:T(8,128)S(1)} async-done(((f32[128,16,128]{2,1,0:T(8,128)}), f32[128,16,128]{2,1,0:T(8,128)S(1)}, u32[]{:S(2)}, u32[]{:S(2)}) %all-to-all-start.1) | async-done | bytes 1048608 | tf_op jit(solution)/shard_map/all_to_all | solution.py:125
  101.1 4.9 %all-to-all-start.3 = ((bf16[32,128,2,256]{3,2,1,0:T(2,128)(2,1)}), bf16[32,128,2,256]{3,2,1,0:T(2,128)(2,1)}, u32[]{:S(2)}, u32[]{:S(2)}) async-start(bf16[32,128,2,256]{3,2,1,0:T(2,128)(2,1)} %gather_fusion), calls=%async_computation.3 | async-start | bytes 8388608 | tf_op jit(solution)/shard_map/all_to_all | solution.py:182
  106.3 5.8 %psum.7 = bf16[16,128]{1,0:T(8,128)(2,1)S(1)} all-reduce(f32[16,128]{1,0:T(8,128)S(1)} %fusion.49), channel_id=1, replica_groups=mesh['groups'=2,'seq'=4,'tensor'=4] {'tensor'}, use_global_device_ids=true, to_apply=%region_12.13 | all-reduce | flops 2048 | bytes 12288 | tf_op jit(solution)/shard_map/psum | solution.py:166
  112.0 0.2 select_reduce_fusion.4
  112.3 0.2 fusion.28
  113.3 0.5 broadcast.339
  113.8 0.7 reduce.4
  114.6 0.7 reduce.3
  115.5 0.3 multiply_reduce_fusion
  116.0 0.7 copy.189
  116.7 80.4 %all-to-all-done.3 = bf16[32,128,2,256]{3,2,1,0:T(2,128)(2,1)} async-done(((bf16[32,128,2,256]{3,2,1,0:T(2,128)(2,1)}), bf16[32,128,2,256]{3,2,1,0:T(2,128)(2,1)}, u32[]{:S(2)}, u32[]{:S(2)}) %all-to-all-start.3) | async-done | bytes 4194336 | tf_op jit(solution)/shard_map/all_to_all | solution.py:182
  197.1 5.0 %copy.157 = bf16[32,128,2,256]{3,1,2,0:T(8,128)(2,1)} copy(bf16[32,128,2,256]{3,2,1,0:T(2,128)(2,1)} %all-to-all-done.3) | data formatting | bytes 8388608 | tf_op jit(solution)/shard_map/all_to_all | solution.py:182
  202.2 4.9 %gather_fusion.1 = bf16[32,128,2,256]{3,1,2,0:T(8,128)(2,1)} fusion(bf16[32,128,2,256]{3,1,2,0:T(8,128)(2,1)} %copy.157, s32[1024]{0:T(1024)S(1)} %pad_clamp_fusion), kind=kCustom, calls=%fused_computation.1 | custom fusion | bytes 8388736 | tf_op jit(solution)/shard_map/gather | solution.py:183
  207.1 2.5 %copy.158 = bf16[32,128,2,256]{3,1,0,2:T(8,128)(2,1)S(1)} copy(bf16[32,128,2,256]{3,1,2,0:T(8,128)(2,1)} %gather_fusion.1) | data formatting | bytes 8388608 | tf_op jit(solution)/shard_map/gather | solution.py:183
  209.5 2.3 fusion.45
  211.8 3.0 %copy.161 = bf16[4,1024,1,256]{1,3,0,2:T(8,128)(2,1)S(1)} copy(bf16[4,1024,1,256]{3,1,0,2:T(8,128)(2,1)} %get-tuple-element.33) | data formatting | bytes 4194304 | tf_op jit(solution)/shard_map/slice | solution.py:184
  214.8 2.6 %copy.162 = bf16[4,1024,2,128]{3,1,2,0:T(8,128)(2,1)} copy(bf16[4,1024,2,128]{1,3,2,0:T(8,128)(2,1)S(1)} %bitcast.125) | data formatting | bytes 4194304 | tf_op jit(solution)/shard_map/concatenate | solution.py:184
  217.4 3.0 %copy.159 = bf16[4,1024,1,256]{1,3,0,2:T(8,128)(2,1)S(1)} copy(bf16[4,1024,1,256]{3,1,0,2:T(8,128)(2,1)} %get-tuple-element.34) | data formatting | bytes 4194304 | tf_op jit(solution)/shard_map/slice | solution.py:185
  220.4 2.6 %copy.160 = bf16[4,1024,2,128]{3,1,2,0:T(8,128)(2,1)} copy(bf16[4,1024,2,128]{1,3,2,0:T(8,128)(2,1)S(1)} %bitcast.126) | data formatting | bytes 4194304 | tf_op jit(solution)/shard_map/concatenate | solution.py:185
  223.0 2.7 %fusion.46 = (f32[4,2,8,4]{2,3,1,0:T(4,128)S(1)}, bf16[4,2,8,4,1028]{4,2,3,1,0:T(8,128)(2,1)S(1)}) fusion(bf16[4,4,2,128]{3,1,2,0:T(4,128)(2,1)S(1)} %bitcast.140, bf16[4,1024,2,128]{3,1,2,0:T(8,128)(2,1)} %copy.162, pred[4,4,1028]{2,1,0:T(4,128)(4,1)S(1)} %pad_add_fusion, bf16[4,4,2,8,128]{4,3,2,1,0:T(8,128)(2,1)S(1)} %reshape.409), kind=kOutput, calls=%fused_computation.96 | convolution fusion | flops 73161728 | bytes 2714688 | tf_op jit(solution)/shard_map/sub | solution.py:37
  225.7 0.5 fusion.18
  226.5 0.7 divide_convert_fusion.1
  (78 shorter events, 2.6 us)
Async XLA Ops:
  0.6 111.7 %copy-start = (bf16[128,2048]{1,0:T(8,128)(2,1)S(1)}, bf16[128,2048]{1,0:T(8,128)(2,1)}, u32[]{:S(2)}) copy-start(bf16[128,2048]{1,0:T(8,128)(2,1)} %param.28) | copy-start | bytes 1572868
  1.9 18.1 %collective-permute-start = (bf16[32,2048]{0,1:T(8,128)(2,1)S(1)}, bf16[32,2048]{0,1:T(8,128)(2,1)}, u32[]{:S(2)}, u32[]{:S(2)}) collective-permute-start(bf16[32,2048]{0,1:T(8,128)(2,1)S(1)} %copy.143), channel_id=1, source_target_pairs={{0,4},{4,8},{8,12},{12,0},{1,5},{5,9},{9,13},{13,1},{2,6},{6,10},{... | collective-permute-start | bytes 393224 | tf_op jit(solution)/shard_map/ppermute | solution.py:96
  5.0 25.0 %collective-permute-start.2 = (bf16[32,2048]{0,1:T(8,128)(2,1)S(1)}, bf16[32,2048]{0,1:T(8,128)(2,1)}, u32[]{:S(2)}, u32[]{:S(2)}) collective-permute-start(bf16[32,2048]{0,1:T(8,128)(2,1)S(1)} %copy.143), channel_id=1, source_target_pairs={{0,12},{4,0},{8,4},{12,8},{1,13},{5,1},{9,5},{13,9},{2,14},{6,2},{... | collective-permute-start | bytes 393224 | tf_op jit(solution)/shard_map/ppermute | solution.py:98
  19.9 21.6 %collective-permute-start.1 = (bf16[32,2048]{0,1:T(8,128)(2,1)}, bf16[32,2048]{0,1:T(8,128)(2,1)}, u32[]{:S(2)}, u32[]{:S(2)}) collective-permute-start(bf16[32,2048]{0,1:T(8,128)(2,1)} %collective-permute-done), channel_id=1, source_target_pairs={{0,4},{4,8},{8,12},{12,0},{1,5},{5,9},{9,13},{13,1},{2,6},{6,10},{... | collective-permute-start | bytes 393224 | tf_op jit(solution)/shard_map/ppermute | solution.py:96
  49.0 4.6 %copy-start.1 = (f32[2,1568,128,8]{2,1,3,0:T(8,128)}, f32[2,1568,128,8]{2,1,3,0:T(8,128)S(1)}, u32[]{:S(2)}) copy-start(f32[2,1568,128,8]{2,1,3,0:T(8,128)S(1)} %get-tuple-element.36) | copy-start | bytes 38535172
  49.0 8.6 %copy-start.3 = (bf16[1536,256]{1,0:T(8,128)(2,1)S(1)}, bf16[1536,256]{1,0:T(8,128)(2,1)}, u32[]{:S(2)}) copy-start(bf16[1536,256]{1,0:T(8,128)(2,1)} %param.21) | copy-start | bytes 2359300
  49.0 8.6 %copy-start.7 = (bf16[32,256]{1,0:T(8,128)(2,1)S(1)}, bf16[32,256]{1,0:T(8,128)(2,1)}, u32[]{:S(2)}) copy-start(bf16[32,256]{1,0:T(8,128)(2,1)} %param.19) | copy-start | bytes 49156
  54.3 8.8 %all-to-all-start.2 = ((f32[4,1,512]{2,1,0:T(1,128)}), f32[4,1,512]{2,1,0:T(1,128)S(1)}, u32[]{:S(2)}, u32[]{:S(2)}) async-start(f32[4,1,512]{2,1,0:T(1,128)} %reshape.433), calls=%async_computation.2 | async-start | bytes 16384 | tf_op jit(solution)/shard_map/all_to_all | solution.py:127
  63.2 11.1 %all-to-all-start = ((f32[4,1,512]{2,1,0:T(1,128)}), f32[4,1,512]{2,1,0:T(1,128)S(1)}, u32[]{:S(2)}, u32[]{:S(2)}) async-start(f32[4,1,512]{2,1,0:T(1,128)} %reshape.431), calls=%async_computation | async-start | bytes 16384 | tf_op jit(solution)/shard_map/all_to_all | solution.py:126
  72.9 6.5 %copy-start.11 = (s32[16]{0:T(128)S(1)}, s32[16]{0:T(128)}, u32[]{:S(2)}) copy-start(s32[16]{0:T(128)} %param.29) | copy-start | bytes 196
  72.9 6.5 %copy-start.8 = (s32[16,8]{0,1:T(8,128)S(1)}, s32[16,8]{0,1:T(8,128)}, u32[]{:S(2)}) copy-start(s32[16,8]{0,1:T(8,128)} %param.30) | copy-start | bytes 1540
  74.3 26.8 %all-to-all-start.1 = ((f32[128,16,128]{2,1,0:T(8,128)}), f32[128,16,128]{2,1,0:T(8,128)S(1)}, u32[]{:S(2)}, u32[]{:S(2)}) async-start(f32[128,16,128]{2,1,0:T(8,128)} %copy.153), calls=%async_computation.1 | async-start | bytes 2097152 | tf_op jit(solution)/shard_map/all_to_all | solution.py:125
  92.7 13.3 %copy-start.5 = (bf16[4,4,2048]{2,1,0:T(4,128)(2,1)S(1)}, bf16[4,4,2048]{2,1,0:T(4,128)(2,1)}, u32[]{:S(2)}) copy-start(bf16[4,4,2048]{2,1,0:T(4,128)(2,1)} %param.26) | copy-start | bytes 196612
  92.7 13.4 %copy-start.4 = (bf16[2048,128]{1,0:T(8,128)(2,1)S(1)}, bf16[2048,128]{1,0:T(8,128)(2,1)}, u32[]{:S(2)}) copy-start(bf16[2048,128]{1,0:T(8,128)(2,1)} %param.27) | copy-start | bytes 1572868
  92.7 19.3 %copy-start.9 = (s32[16]{0:T(128)S(1)}, s32[16]{0:T(128)}, u32[]{:S(2)}) copy-start(s32[16]{0:T(128)} %param.32) | copy-start | bytes 196
  92.7 19.3 %copy-start.10 = (s32[16]{0:T(128)S(1)}, s32[16]{0:T(128)}, u32[]{:S(2)}) copy-start(s32[16]{0:T(128)} %param.33) | copy-start | bytes 196
  92.7 19.8 %copy-start.6 = (bf16[4,4,2048]{2,1,0:T(4,128)(2,1)S(1)}, bf16[4,4,2048]{2,1,0:T(4,128)(2,1)}, u32[]{:S(2)}) copy-start(bf16[4,4,2048]{2,1,0:T(4,128)(2,1)} %param.23) | copy-start | bytes 196612
  92.7 19.9 %copy-start.14 = (s32[16]{0:T(128)S(1)}, s32[16]{0:T(128)}, u32[]{:S(2)}) copy-start(s32[16]{0:T(128)} %param.31) | copy-start | bytes 196
  101.1 96.0 %all-to-all-start.3 = ((bf16[32,128,2,256]{3,2,1,0:T(2,128)(2,1)}), bf16[32,128,2,256]{3,2,1,0:T(2,128)(2,1)}, u32[]{:S(2)}, u32[]{:S(2)}) async-start(bf16[32,128,2,256]{3,2,1,0:T(2,128)(2,1)} %gather_fusion), calls=%async_computation.3 | async-start | bytes 8388608 | tf_op jit(solution)/shard_map/all_to_all | solution.py:182
  217.4 5.6 %copy-start.12 = (bf16[4,4,256]{2,1,0:T(4,128)(2,1)S(1)}, bf16[4,4,256]{2,1,0:T(4,128)(2,1)}, u32[]{:S(2)}) copy-start(bf16[4,4,256]{2,1,0:T(4,128)(2,1)} %param.24) | copy-start | bytes 24580
  223.0 2.7 %copy-start.2 = (bf16[4,1024,2,128]{3,1,2,0:T(8,128)(2,1)S(1)}, bf16[4,1024,2,128]{3,1,2,0:T(8,128)(2,1)}, u32[]{:S(2)}) copy-start(bf16[4,1024,2,128]{3,1,2,0:T(8,128)(2,1)} %copy.160) | copy-start | bytes 6291460
  223.0 2.7 %copy-start.13 = (bf16[4,4,256]{2,1,0:T(4,128)(2,1)S(1)}, bf16[4,4,256]{2,1,0:T(4,128)(2,1)}, u32[]{:S(2)}) copy-start(bf16[4,4,256]{2,1,0:T(4,128)(2,1)} %param.25) | copy-start | bytes 24580
